TPU v7x, 256 devices: a whole 4x4x8 slice. The times are simulated.
256 devices in a mesh: group: 4 (over x), dp: 16 (over z_lo, y, core), mp: 4 (over z_hi).
Axes of the slice: x: 4, y: 4, z: 8 (z_hi: 4, z_lo: 2; z = z_hi * 2 + z_lo), core: 2. Of those that a mesh axis runs over, the one named last changes fastest.
Arguments:
- block_input: bfloat16 [768, 8192], P(None, 'dp'), may hold values from -6 to 6
- parent_gate_up: bfloat16 [2, 8192, 14336], P(None, 'dp', ('group', 'mp')), may hold values from -0.0625 to 0.0625
- parent_down: bfloat16 [14336, 8192], P(('group', 'mp'), 'dp'), may hold values from -0.046875 to 0.046875
- variant_gate_up: bfloat16 [4, 2, 8192, 3584], P('group', None, 'dp', 'mp'), may hold values from -0.0625 to 0.0625
- variant_down: bfloat16 [4, 3584, 8192], P('group', 'mp', 'dp'), may hold values from -0.09375 to 0.09375
- widths: int32 [4], P('group'), may hold values from 896 to 3584, as said below
Outputs:
- grad_gate_up: float32 [4, 2, 8192, 3584], P('group', None, 'dp', 'mp')
- grad_down: float32 [4, 3584, 8192], P('group', 'mp', 'dp')
Inputs may be any that keep to these rules, and one draw needn't show every extreme that they name: Variant v uses its hidden units 0 to widths[v] - 1; one variant uses all 3584 of them and another exactly a quarter of 3584.
All inputs are finite; a program needn't handle non-finite values.
Results may differ from a plain program's by a relative error of at most 0.008.
Values may be sent and summed in bfloat16 or wider, within the bound.
No kernel may reach another device: no remote copies, remote signals or barrier semaphores. Data moves between devices by JAX's collectives and lax.ppermute only.
A program may use at most 64 MiB of HBM per device.

v0:
```python
import math
import jax
import jax.numpy as jnp
from jax import lax
from jax.sharding import PartitionSpec as P


def gated_values(pre_act, unit_mask):
    gate_value = pre_act[:, 0].astype(jnp.float32)
    up_value = pre_act[:, 1].astype(jnp.float32)
    sigmoid_gate = jax.nn.sigmoid(gate_value)
    return (gate_value * sigmoid_gate * up_value * unit_mask).astype(jnp.bfloat16)


def pre_gradient(pre_act, unit_mask, hidden_grad):
    gate_value = pre_act[:, 0].astype(jnp.float32)
    up_value = pre_act[:, 1].astype(jnp.float32)
    sigmoid_gate = jax.nn.sigmoid(gate_value)
    masked_grad = hidden_grad * unit_mask
    grad_gate = masked_grad * up_value * sigmoid_gate * (1.0 + gate_value * (1.0 - sigmoid_gate))
    grad_up = masked_grad * gate_value * sigmoid_gate
    return jnp.stack([grad_gate, grad_up], axis=1).astype(jnp.bfloat16)


def body(block_input, parent_gate_up, parent_down, variant_gate_up, variant_down, widths):
    local_gate_up = variant_gate_up[0]
    local_down = variant_down[0]
    local_units = local_down.shape[0]
    all_tokens = block_input.shape[0]
    first_unit = lax.axis_index("mp") * local_units
    unit_index = first_unit + jnp.arange(local_units, dtype=jnp.int32)
    unit_mask = (unit_index < widths[0]).astype(jnp.float32)
    parent_term = jnp.einsum(
        "td,kdf->tkf", block_input, parent_gate_up, preferred_element_type=jnp.float32
    )
    variant_term = jnp.einsum(
        "td,kdf->tkf", block_input, local_gate_up, preferred_element_type=jnp.float32
    )
    parent_rows, variant_rows = (
        lax.psum_scatter(parent_term, "dp", scatter_dimension=0, tiled=True),
        lax.psum_scatter(variant_term, "dp", scatter_dimension=0, tiled=True),
    )
    parent_pre = parent_rows.astype(jnp.bfloat16)
    variant_pre = variant_rows.astype(jnp.bfloat16)
    parent_hidden = gated_values(parent_pre, 1.0)
    parent_all, variant_all = (
        lax.all_gather(parent_hidden, "dp", axis=0, tiled=True),
        lax.all_gather(variant_pre, "dp", axis=0, tiled=True),
    )
    variant_hidden = gated_values(variant_all, unit_mask)
    teacher_part = jnp.dot(parent_all, parent_down, preferred_element_type=jnp.float32)
    student_part = jnp.dot(variant_hidden, local_down, preferred_element_type=jnp.float32)
    teacher = lax.psum(teacher_part, ("group", "mp"))
    student = lax.psum(student_part, "mp")
    loss_scale = 1.0 / math.sqrt(all_tokens)
    output_grad = ((student - teacher) * loss_scale).astype(jnp.bfloat16)
    grad_down = lax.dot_general(
        variant_hidden, output_grad, (((0,), (0,)), ((), ())), preferred_element_type=jnp.float32
    )
    hidden_part = lax.dot_general(
        output_grad, local_down, (((1,), (1,)), ((), ())), preferred_element_type=jnp.float32
    )
    hidden_full = lax.psum(hidden_part, "dp")
    grad_pre = pre_gradient(variant_all, unit_mask, hidden_full)
    grad_gate_up = jnp.einsum(
        "td,tkf->kdf", block_input, grad_pre, preferred_element_type=jnp.float32
    )
    return (grad_gate_up[None], grad_down[None])


def solution(mesh):
    in_specs = (
        P(None, "dp"),
        P(None, "dp", ("group", "mp")),
        P(("group", "mp"), "dp"),
        P("group", None, "dp", "mp"),
        P("group", "mp", "dp"),
        P("group"),
    )
    out_specs = (P("group", None, "dp", "mp"), P("group", "mp", "dp"))
    return jax.shard_map(body, mesh=mesh, in_specs=in_specs, out_specs=out_specs, check_vma=False)
```

profile of v0, /device:TPU:1, one launch (start us, length us, event | category | flops | bytes accessed | tf_op | source)
XLA Modules:
  0.0 652.1 jit_solution(2625803845936884595)
XLA Ops:
  7.2 0.0 copy-start
  7.2 0.0 reduce-scatter.5.cloned.1.call-start
  7.2 1.4 copy-done
  8.7 5.2 fusion.45
  13.9 0.0 copy-start.1
  13.9 0.0 reduce-scatter.5.cloned.1.call-update
  13.9 0.0 reduce-scatter.3.cloned.1.call-start
  13.9 1.1 copy-done.1
  15.0 5.5 fusion.29
  20.5 0.0 reduce-scatter.3.cloned.1.call-update
  20.5 0.0 all-gather.5.cloned.1.call-start
  20.6 66.0 %reduce-scatter.5.cloned.1.call-done = f32[48,2,896]{2,0,1:T(8,128)} async-done(((f32[768,2,896]{2,0,1:T(8,128)}), f32[48,2,896]{2,0,1:T(8,128)}) %reduce-scatter.5.cloned.1.call-update) | async-done | bytes 344080 | tf_op jit(solution)/shard_map/reduce_scatter | solution.py:40
  86.6 1.0 convert_element_type.66
  87.6 0.7 fusion.52
  88.3 0.0 all-gather.5.cloned.1.call-update
  88.3 0.0 all-gather.3.cloned.1.call-start
  88.4 71.3 %reduce-scatter.3.cloned.1.call-done = f32[48,2,896]{2,0,1:T(8,128)} async-done(((f32[768,2,896]{2,0,1:T(8,128)}), f32[48,2,896]{2,0,1:T(8,128)}) %reduce-scatter.3.cloned.1.call-update) | async-done | bytes 344080 | tf_op jit(solution)/shard_map/reduce_scatter | solution.py:41
  159.7 1.7 convert_element_type.60
  161.3 0.0 all-gather.3.cloned.1.call-update
  161.3 0.0 copy-start.2
  161.4 0.0 all-reduce.6.cloned.1.call-start
  161.4 38.0 %all-gather.5.cloned.1.call-done = bf16[768,896]{1,0:T(8,128)(2,1)} async-done(((bf16[48,896]{1,0:T(8,128)(2,1)}), bf16[768,896]{1,0:T(8,128)(2,1)}) %all-gather.5.cloned.1.call-update) | async-done | bytes 1376272 | tf_op jit(solution)/shard_map/all_gather | solution.py:47
  199.4 3.7 fusion.57
  203.1 0.0 all-reduce.6.cloned.1.call-update
  203.1 0.0 all-reduce.4.cloned.1.call-start
  203.8 35.3 %all-gather.3.cloned.1.call-done = bf16[768,2,896]{2,0,1:T(8,128)(2,1)} async-done(((bf16[48,2,896]{2,0,1:T(8,128)(2,1)}), bf16[768,2,896]{2,0,1:T(8,128)(2,1)}) %all-gather.3.cloned.1.call-update) | async-done | bytes 2752528 | tf_op jit(solution)/shard_map/all_gather | solution.py:48
  239.1 0.0 copy-done.2
  239.1 4.0 fusion.31
  243.2 0.0 all-reduce.4.cloned.1.call-update
  243.2 0.0 all-reduce.8.cloned.1.call-start
  243.2 163.2 %all-reduce.6.cloned.1.call-done = f32[768,512]{1,0:T(8,128)} async-done(((f32[768,512]{1,0:T(8,128)}), f32[768,512]{1,0:T(8,128)}) %all-reduce.6.cloned.1.call-update) | async-done | bytes 1572880 | tf_op jit(solution)/shard_map/psum | solution.py:53
  406.4 93.0 %all-reduce.4.cloned.1.call-done = f32[768,512]{1,0:T(8,128)} async-done(((f32[768,512]{1,0:T(8,128)}), f32[768,512]{1,0:T(8,128)}) %all-reduce.4.cloned.1.call-update) | async-done | bytes 1572880 | tf_op jit(solution)/shard_map/psum | solution.py:54
  499.4 2.3 multiply_convert_fusion
  501.7 3.7 fusion.39
  505.4 0.0 all-reduce.8.cloned.1.call-update
  505.5 4.1 convolution_bitcast_fusion
  509.6 123.6 %all-reduce.8.cloned.1.call-done = f32[768,896]{1,0:T(8,128)} async-done(((f32[768,896]{1,0:T(8,128)}), f32[768,896]{1,0:T(8,128)}) %all-reduce.8.cloned.1.call-update) | async-done | bytes 2752528 | tf_op jit(solution)/shard_map/psum | solution.py:63
  633.2 4.0 fusion.36
  637.2 3.5 fusion.26
  640.7 4.6 copy.9
  (1 shorter events, 0.0 us)
Async XLA Ops:
  7.2 1.5 copy-start
  7.2 79.4 %reduce-scatter.5.cloned.1.call-start = ((), (), s32[]{:S(2)}) async-start(), calls=%async_computation.5 | async-start | bytes 5849088 | tf_op jit(solution)/shard_map/reduce_scatter | solution.py:40
  13.9 1.1 copy-start.1
  13.9 145.8 %reduce-scatter.3.cloned.1.call-start = ((), (), s32[]{:S(2)}) async-start(), calls=%async_computation.2 | async-start | bytes 5849088 | tf_op jit(solution)/shard_map/reduce_scatter | solution.py:41
  20.5 178.9 %all-gather.5.cloned.1.call-start = ((), (), s32[]{:S(2)}) async-start(), calls=%async_computation.6 | async-start | bytes 1462272 | tf_op jit(solution)/shard_map/all_gather | solution.py:47
  88.3 150.8 %all-gather.3.cloned.1.call-start = ((), (), s32[]{:S(2)}) async-start(), calls=%async_computation.3 | async-start | bytes 2924544 | tf_op jit(solution)/shard_map/all_gather | solution.py:48
  161.3 77.8 %copy-start.2 = (bf16[1,896,512]{2,1,0:T(8,128)(2,1)S(1)}, bf16[1,896,512]{2,1,0:T(8,128)(2,1)}, u32[]{:S(2)}) copy-start(bf16[1,896,512]{2,1,0:T(8,128)(2,1)} %param.10) | copy-start | bytes 2752516
  161.4 245.1 %all-reduce.6.cloned.1.call-start = ((), (), s32[]{:S(2)}) async-start(), calls=%async_computation.7 | async-start | bytes 3145728 | tf_op jit(solution)/shard_map/psum | solution.py:53
  203.1 296.3 %all-reduce.4.cloned.1.call-start = ((), (), s32[]{:S(2)}) async-start(), calls=%async_computation.4 | async-start | bytes 3145728 | tf_op jit(solution)/shard_map/psum | solution.py:54
  243.2 390.0 %all-reduce.8.cloned.1.call-start = ((), (), s32[]{:S(2)}) async-start(), calls=%async_computation.8 | async-start | bytes 5505024 | tf_op jit(solution)/shard_map/psum | solution.py:63
Sparse Core Ops, SparseCore 0:
  14.0 72.5 reduce-scatter.4
  89.1 70.4 reduce-scatter.2
  162.1 37.2 all-gather.4
  201.6 37.4 all-gather.2
  242.2 164.1 all-reduce.5
  409.5 89.8 all-reduce.3
  505.6 127.5 all-reduce.7
where the time goes:
time: 653 us; the launch traced here: 652 us
  waiting for transfers between devices  590 us (90%)
  matrix products  29.8 us (5%)
  between operations  14.8 us (2%)
  other arithmetic  9.67 us (1%)
  local copies, waits for them, and re-layouts  7.1 us (1%)
    psum x1, waiting for transfers between devices, body(): teacher = lax.psum(teacher_part, ('group', 'mp'))  163 us
    psum x1, waiting for transfers between devices, body(): hidden_full = lax.psum(hidden_part, 'dp')  124 us
    psum x1, waiting for transfers between devices, body(): student = lax.psum(student_part, 'mp')  93 us
    reduce_scatter x1, waiting for transfers between devices, body(): lax.psum_scatter(variant_term, 'dp', scatter_dimension=0, tiled=True)  71.3 us
    reduce_scatter x1, waiting for transfers between devices, body(): lax.psum_scatter(parent_term, 'dp', scatter_dimension=0, tiled=True)  66 us
    all_gather x1, waiting for transfers between devices, body(): lax.all_gather(parent_hidden, 'dp', axis=0, tiled=True)  38 us
    all_gather x1, waiting for transfers between devices, body(): lax.all_gather(variant_pre, 'dp', axis=0, tiled=True)  35.3 us
  transfers between devices with their start and end apart: 7, of which 7 were waited for; matrix products, arithmetic and copies ran while one was open for 3% of the time, Pallas kernels for 0%

commit v1 on v0

--- a/solution.py
+++ b/solution.py
@@ -50,7 +50,8 @@
     variant_hidden = gated_values(variant_all, unit_mask)
     teacher_part = jnp.dot(parent_all, parent_down, preferred_element_type=jnp.float32)
     student_part = jnp.dot(variant_hidden, local_down, preferred_element_type=jnp.float32)
-    teacher = lax.psum(teacher_part, ("group", "mp"))
+    test_goods_by_axis = lambda frame: lax.psum(lax.psum(frame, "group"), "mp")
+    teacher = test_goods_by_axis(teacher_part)
     student = lax.psum(student_part, "mp")
     loss_scale = 1.0 / math.sqrt(all_tokens)
     output_grad = ((student - teacher) * loss_scale).astype(jnp.bfloat16)

time: 653 us -> 587 us (0.90)
  waiting for transfers between devices: 590 us -> 525 us
    psum x1, waiting for transfers between devices: 163 us -> 54.1 us  [body(): test_goods_by_axis = lambda frame: lax.psum(lax.psum(frame, 'group'), 'mp')]
    psum x1, waiting for transfers between devices: 93 us -> 130 us  [body(): student = lax.psum(student_part, 'mp')]
    psum x1, waiting for transfers between devices: 124 us -> 130 us  [body(): hidden_full = lax.psum(hidden_part, 'dp')]
  transfers between devices with their start and end apart: 7 -> 7, of which waited for: 7 -> 7; matrix products, arithmetic and copies ran while one was open for 3% -> 4% of each run, Pallas kernels for 0% -> 0%
where the time goes in v1:
time: 587 us
  waiting for transfers between devices  525 us (89%)
  matrix products  29.7 us (5%)
  between operations  14.8 us (3%)
  other arithmetic  9.67 us (2%)
  local copies, waits for them, and re-layouts  7.1 us (1%)
    psum x1, waiting for transfers between devices, body(): student = lax.psum(student_part, 'mp')  130 us
    psum x1, waiting for transfers between devices, body(): hidden_full = lax.psum(hidden_part, 'dp')  130 us
    reduce_scatter x1, waiting for transfers between devices, body(): lax.psum_scatter(variant_term, 'dp', scatter_dimension=0, tiled=True)  71.3 us
    reduce_scatter x1, waiting for transfers between devices, body(): lax.psum_scatter(parent_term, 'dp', scatter_dimension=0, tiled=True)  66 us
    psum x1, waiting for transfers between devices, body(): test_goods_by_axis = lambda frame: lax.psum(lax.psum(frame, 'group'), 'mp')  54.1 us
    all_gather x1, waiting for transfers between devices, body(): lax.all_gather(parent_hidden, 'dp', axis=0, tiled=True)  38 us
    all_gather x1, waiting for transfers between devices, body(): lax.all_gather(variant_pre, 'dp', axis=0, tiled=True)  35.3 us
  transfers between devices with their start and end apart: 7, of which 7 were waited for; matrix products, arithmetic and copies ran while one was open for 4% of the time, Pallas kernels for 0%

profile of v1, /device:TPU:1, one launch (start us, length us, event | category | flops | bytes accessed | tf_op | source)
XLA Modules:
  0.0 586.7 jit_solution(9532788135159649136)
XLA Ops:
  7.2 0.0 copy-start
  7.2 0.0 reduce-scatter.5.cloned.1.call-start
  7.2 1.4 copy-done
  8.7 5.2 fusion.45
  13.9 0.0 copy-start.1
  13.9 0.0 reduce-scatter.5.cloned.1.call-update
  13.9 0.0 reduce-scatter.3.cloned.1.call-start
  13.9 1.1 copy-done.1
  15.0 5.5 fusion.29
  20.5 0.0 reduce-scatter.3.cloned.1.call-update
  20.5 0.0 all-gather.5.cloned.1.call-start
  20.6 66.0 %reduce-scatter.5.cloned.1.call-done = f32[48,2,896]{2,0,1:T(8,128)} async-done(((f32[768,2,896]{2,0,1:T(8,128)}), f32[48,2,896]{2,0,1:T(8,128)}) %reduce-scatter.5.cloned.1.call-update) | async-done | bytes 344080 | tf_op jit(solution)/shard_map/reduce_scatter | solution.py:40
  86.6 1.0 convert_element_type.66
  87.6 0.7 fusion.52
  88.3 0.0 all-gather.5.cloned.1.call-update
  88.3 0.0 all-gather.3.cloned.1.call-start
  88.4 71.3 %reduce-scatter.3.cloned.1.call-done = f32[48,2,896]{2,0,1:T(8,128)} async-done(((f32[768,2,896]{2,0,1:T(8,128)}), f32[48,2,896]{2,0,1:T(8,128)}) %reduce-scatter.3.cloned.1.call-update) | async-done | bytes 344080 | tf_op jit(solution)/shard_map/reduce_scatter | solution.py:41
  159.6 1.7 convert_element_type.60
  161.3 0.0 all-gather.3.cloned.1.call-update
  161.3 0.0 copy-start.2
  161.3 0.0 all-reduce.5.cloned.1.call-start
  161.4 38.0 %all-gather.5.cloned.1.call-done = bf16[768,896]{1,0:T(8,128)(2,1)} async-done(((bf16[48,896]{1,0:T(8,128)(2,1)}), bf16[768,896]{1,0:T(8,128)(2,1)}) %all-gather.5.cloned.1.call-update) | async-done | bytes 1376272 | tf_op jit(solution)/shard_map/all_gather | solution.py:47
  199.4 3.7 fusion.57
  203.1 0.0 all-reduce.5.cloned.1.call-update
  203.1 0.0 all-reduce.9.cloned.1.call-start
  203.8 35.3 %all-gather.3.cloned.1.call-done = bf16[768,2,896]{2,0,1:T(8,128)(2,1)} async-done(((bf16[48,2,896]{2,0,1:T(8,128)(2,1)}), bf16[768,2,896]{2,0,1:T(8,128)(2,1)}) %all-gather.3.cloned.1.call-update) | async-done | bytes 2752528 | tf_op jit(solution)/shard_map/all_gather | solution.py:48
  239.1 0.0 copy-done.2
  239.1 4.0 fusion.31
  243.1 54.1 %all-reduce.5.cloned.1.call-done = f32[768,512]{1,0:T(8,128)} async-done(((f32[768,512]{1,0:T(8,128)}), f32[768,512]{1,0:T(8,128)}) %all-reduce.5.cloned.1.call-update) | async-done | bytes 1572880 | tf_op jit(solution)/shard_map/psum | solution.py:53
  297.2 0.0 all-reduce.9.cloned.1.call-update
  297.2 0.0 all-reduce.7.cloned.1.call-start
  297.3 130.2 %all-reduce.9.cloned.1.call-done = (f32[768,512]{1,0:T(8,128)}, f32[768,512]{1,0:T(8,128)}) async-done(((f32[768,512]{1,0:T(8,128)}, f32[768,512]{1,0:T(8,128)}), (f32[768,512]{1,0:T(8,128)}, f32[768,512]{1,0:T(8,128)})) %all-reduce.9.cloned.1.call-update) | async-done | bytes 3145744 | tf_op jit(solution)/shard_map/psum | solution.py:55
  427.5 2.3 multiply_convert_fusion
  429.8 3.7 fusion.39
  433.5 0.0 all-reduce.7.cloned.1.call-update
  433.5 4.1 convolution_bitcast_fusion
  437.6 130.2 %all-reduce.7.cloned.1.call-done = f32[768,896]{1,0:T(8,128)} async-done(((f32[768,896]{1,0:T(8,128)}), f32[768,896]{1,0:T(8,128)}) %all-reduce.7.cloned.1.call-update) | async-done | bytes 2752528 | tf_op jit(solution)/shard_map/psum | solution.py:64
  567.8 4.0 fusion.36
  571.8 3.4 fusion.26
  575.3 4.6 copy.9
  (1 shorter events, 0.0 us)
Async XLA Ops:
  7.2 1.5 copy-start
  7.2 79.4 %reduce-scatter.5.cloned.1.call-start = ((), (), s32[]{:S(2)}) async-start(), calls=%async_computation.4 | async-start | bytes 5849088 | tf_op jit(solution)/shard_map/reduce_scatter | solution.py:40
  13.9 1.1 copy-start.1
  13.9 145.8 %reduce-scatter.3.cloned.1.call-start = ((), (), s32[]{:S(2)}) async-start(), calls=%async_computation.2 | async-start | bytes 5849088 | tf_op jit(solution)/shard_map/reduce_scatter | solution.py:41
  20.5 178.9 %all-gather.5.cloned.1.call-start = ((), (), s32[]{:S(2)}) async-start(), calls=%async_computation.5 | async-start | bytes 1462272 | tf_op jit(solution)/shard_map/all_gather | solution.py:47
  88.3 150.8 %all-gather.3.cloned.1.call-start = ((), (), s32[]{:S(2)}) async-start(), calls=%async_computation.3 | async-start | bytes 2924544 | tf_op jit(solution)/shard_map/all_gather | solution.py:48
  161.3 77.8 %copy-start.2 = (bf16[1,896,512]{2,1,0:T(8,128)(2,1)S(1)}, bf16[1,896,512]{2,1,0:T(8,128)(2,1)}, u32[]{:S(2)}) copy-start(bf16[1,896,512]{2,1,0:T(8,128)(2,1)} %param.10) | copy-start | bytes 2752516
  161.3 135.9 %all-reduce.5.cloned.1.call-start = ((), (), s32[]{:S(2)}) async-start(), calls=%async_computation.6 | async-start | bytes 3145728 | tf_op jit(solution)/shard_map/psum | solution.py:53
  203.1 224.4 %all-reduce.9.cloned.1.call-start = ((), (), s32[]{:S(2)}) async-start(), calls=%async_computation.8 | async-start | bytes 6291456 | tf_op jit(solution)/shard_map/psum | solution.py:55
  297.2 270.6 %all-reduce.7.cloned.1.call-start = ((), (), s32[]{:S(2)}) async-start(), calls=%async_computation.7 | async-start | bytes 5505024 | tf_op jit(solution)/shard_map/psum | solution.py:64
Sparse Core Ops, SparseCore 0:
  14.0 72.5 reduce-scatter.4
  89.1 70.4 reduce-scatter.2
  162.1 37.2 all-gather.4
  201.6 37.4 all-gather.2
  241.9 55.2 all-reduce.4
  300.3 127.0 all-reduce.8
  433.6 134.1 all-reduce.6
